TPU v7x, 512 devices: a whole 4x4x16 slice. The times are simulated.
512 devices in a mesh: dp: 64 (over y, z), mp: 8 (over x, core).
Axes of the slice: x: 4, y: 4, z: 16, core: 2. Of those that a mesh axis runs over, the one named last changes fastest.
Arguments:
- tokens: bfloat16 [512, 8192], P('mp', 'dp'), may hold values from -6 to 6
- norm_gain: float32 [8192], replicated, may hold values from 0.25 to 1.75
- query_weight: bfloat16 [8192, 8192], P(None, 'dp'), may hold values from -0.0625 to 0.0625
- out_weight: bfloat16 [8192, 8192], P(None, 'dp'), may hold values from -0.0625 to 0.0625
- gate_scalar: float32 [1], replicated, may hold values from 0.4 to 1.5
- image_keys: bfloat16 [128, 64, 8192], P('mp', None, 'dp'), may hold values from -260 to 260
- image_values: bfloat16 [128, 64, 8192], P('mp', None, 'dp'), may hold values from -6 to 6
- active_image: int32 [128, 4], replicated, may hold values from 0 to 127
- image_slot: int32 [128], replicated, may hold values from 0 to 127, each once
Outputs:
- mixed: bfloat16 [512, 8192], P('mp', 'dp')
Inputs may be any that keep to these rules, and one draw needn't show every extreme that they name: `image_slot`: each slot 0 to 127 once.
All inputs are finite; a program needn't handle non-finite values.
Results may differ from a plain program's by a relative error of at most 0.0047.
Values may be sent and summed in bfloat16 or wider, within the bound.
A program may use at most 64 MiB of HBM per device.

v0:
```python
import jax
import jax.numpy as jnp
from jax import lax
from jax.sharding import Mesh
from jax.sharding import PartitionSpec as P

DP = ("dp_0", "dp_1")


epsilon = 1e-05


def laid_out(parts, dim):
    lengths = list(parts.shape[1:])
    lengths[dim] *= parts.shape[0]
    return jnp.moveaxis(parts, 0, dim).reshape(lengths)


def gather_in_order(value, axes, sequence):
    parts = value[None]
    for k in sequence:
        parts = lax.all_gather(parts, axes[k], axis=0, tiled=True)
    carried = [lax.axis_size(axes[k]) for k in reversed(sequence)]
    parts = parts.reshape(*carried, *value.shape)
    turned = sorted(range(len(sequence)), key=lambda place: sequence[len(sequence) - 1 - place])
    return parts.transpose(*turned, *range(len(sequence), parts.ndim)).reshape(-1, *value.shape)


def whole_of(value, axes, sequence, dim):
    return laid_out(gather_in_order(value, axes, sequence), dim)


def from_everyone(value, axis):
    copies = jnp.broadcast_to(value, (lax.axis_size(axis), *value.shape))
    return lax.all_to_all(copies, axis, split_axis=0, concat_axis=0, tiled=True)


def gathered_copies(value, axis, dim):
    parts = from_everyone(value, axis)
    return laid_out(parts, dim)


def split_up(value, dim, peers):
    lengths = value.shape
    parts = value.reshape(*lengths[:dim], peers, lengths[dim] // peers, *lengths[dim + 1 :])
    return jnp.moveaxis(parts, dim, 0)


def sent_and_summed(value, axis, dim):
    peers = lax.axis_size(axis)
    parts = lax.all_to_all(split_up(value, dim, peers), axis, 0, 0, tiled=True)
    return jnp.sum(parts.astype(jnp.float32), axis=0)


def attend(queries, wanted, keys_block, values_block, first_slot):
    visual = keys_block.shape[1]
    width = keys_block.shape[2]
    flat_keys = keys_block.reshape(-1, width)
    flat_values = values_block.reshape(-1, width)
    scores = lax.dot_general(
        queries, flat_keys, (((1,), (1,)), ((), ())), preferred_element_type=jnp.float32
    ) * width ** (-0.5)
    column_slot = first_slot + jnp.arange(flat_keys.shape[0], dtype=jnp.int32) // visual
    matches = wanted[:, None] == column_slot[None, :]
    owned = jnp.any(matches, axis=1, keepdims=True)
    masked = jnp.where(matches, scores, -1e30)
    largest = jnp.max(masked, axis=1, keepdims=True)
    expo = jnp.where(matches, jnp.exp(masked - largest), 0.0)
    totals = jnp.where(owned, jnp.sum(expo, axis=1, keepdims=True), 1.0)
    rounded = (expo / totals).astype(jnp.bfloat16)
    result = jnp.dot(rounded, flat_values, preferred_element_type=jnp.float32)
    return jnp.where(owned, result, 0.0)


def body(
    tokens,
    norm_gain,
    query_weight,
    out_weight,
    gate_scalar,
    image_keys,
    image_values,
    active_image,
    image_slot,
):
    whole = whole_of(tokens, DP, (0, 1), 1)
    widened = whole.astype(jnp.float32)
    average = jnp.mean(widened, axis=1, keepdims=True)
    centred = widened - average
    variance = jnp.mean(centred * centred, axis=1, keepdims=True)
    normed = (centred * lax.rsqrt(variance + epsilon) * norm_gain).astype(jnp.bfloat16)
    queries = jnp.dot(normed, query_weight, preferred_element_type=jnp.float32).astype(jnp.bfloat16)
    slots_all = image_slot[active_image.reshape(-1)]
    owned_slots = image_keys.shape[0]
    every_query = gathered_copies(queries, "mp", 0)
    first_slot = lax.axis_index("mp") * owned_slots
    gathered = sent_and_summed(
        attend(every_query, slots_all, image_keys, image_values, first_slot).astype(jnp.bfloat16),
        "mp",
        0,
    )
    attended = gathered.astype(jnp.bfloat16)
    projected = jnp.dot(
        whole_of(attended, DP, (0, 1), 1), out_weight, preferred_element_type=jnp.float32
    )
    result = tokens.astype(jnp.float32) + jnp.tanh(gate_scalar[0]) * projected
    return result.astype(jnp.bfloat16)


def solution(mesh):
    split = Mesh(mesh.devices.reshape(4, 16, mesh.shape["mp"]), ("dp_0", "dp_1", "mp"))
    placed = (
        P("mp", DP),
        P(),
        P(None, DP),
        P(None, DP),
        P(),
        P("mp", None, DP),
        P("mp", None, DP),
        P(),
        P(),
    )
    return jax.shard_map(body, mesh=split, in_specs=placed, out_specs=P("mp", DP), check_vma=False)
```

profile of v0, /device:TPU:2, one launch (start us, length us, event | category | flops | bytes accessed | tf_op | source)
XLA Modules:
  0.0 209.5 jit_solution(14668221166612236900)
XLA Ops:
  6.5 0.0 copy-start
  6.5 0.0 all-gather.5.cloned.1.call-start
  6.5 14.0 %all-gather = bf16[256,128]{1,0:T(8,128)(2,1)} all-gather(bf16[64,128]{1,0:T(8,128)(2,1)} %param.9), channel_id=2, replica_groups=mesh['dp_0'=4,'dp_1'=16,'mp'=8] {'dp_0'}, dimensions={0}, use_global_device_ids=true | all-gather | bytes 81920 | tf_op jit(solution)/shard_map/all_gather | solution.py:22
  20.6 0.0 all-gather.5.cloned.1.call-update
  20.6 0.8 copy.18
  21.4 0.1 reshape.104
  21.5 3.4 %gather_fusion = s32[512]{0:T(512)S(1)} fusion(s32[128]{0:T(128)} %param.17, s32[1024]{0:T(1024)S(1)} %pad_clamp_fusion), kind=kCustom, calls=%fused_computation | custom fusion | bytes 6144 | tf_op jit(solution)/shard_map/gather | solution.py:93
  25.0 69.7 %all-gather.5.cloned.1.call-done = bf16[64,64,128]{2,1,0:T(8,128)(2,1)} async-done(((bf16[4,64,128]{2,1,0:T(8,128)(2,1)}), bf16[64,64,128]{2,1,0:T(8,128)(2,1)}) %all-gather.5.cloned.1.call-update) | async-done | bytes 1048592 | tf_op jit(solution)/shard_map/all_gather | solution.py:22
  94.6 1.5 convert_reduce_fusion
  96.1 1.5 convert_element_type.65
  97.6 0.2 copy.19
  97.9 0.0 copy-start.3
  97.9 0.4 fusion.4
  98.3 0.0 copy-done
  98.3 0.3 copy-done.3
  98.6 0.0 copy-start.4
  98.6 0.6 convolution_convert_fusion
  99.2 0.7 broadcast_in_dim.43
  99.9 4.8 %all-to-all-start = ((bf16[8,64,128]{2,1,0:T(8,128)(2,1)}), bf16[8,64,128]{2,1,0:T(8,128)(2,1)S(1)}, u32[]{:S(2)}, u32[]{:S(2)}) async-start(bf16[8,64,128]{2,1,0:T(8,128)(2,1)} %broadcast_in_dim.43), calls=%async_computation | async-start | bytes 262144 | tf_op jit(solution)/shard_map/all_to_all | solution.py:35
  104.7 0.0 all-gather.7.cloned.1.call-start
  104.7 0.4 compare_reduce_fusion
  105.1 4.3 %all-to-all-done = bf16[8,64,128]{2,1,0:T(8,128)(2,1)S(1)} async-done(((bf16[8,64,128]{2,1,0:T(8,128)(2,1)}), bf16[8,64,128]{2,1,0:T(8,128)(2,1)S(1)}, u32[]{:S(2)}, u32[]{:S(2)}) %all-to-all-start) | async-done | bytes 131104 | tf_op jit(solution)/shard_map/all_to_all | solution.py:35
  109.3 0.0 copy-done.4
  109.3 0.0 copy-start.5
  109.3 0.5 fusion.5
  109.9 0.7 fusion.6
  110.6 0.0 copy-done.5
  110.6 1.2 fusion.7
  111.8 0.0 copy-start.2
  111.8 8.5 %all_to_all.10 = bf16[8,64,128]{2,1,0:T(8,128)(2,1)S(1)} all-to-all(bf16[8,64,128]{2,1,0:T(8,128)(2,1)S(1)} %bitcast.51), channel_id=1, replica_groups=mesh['dp_0'=4,'dp_1'=16,'mp'=8] {'mp'}, dimensions={0} | all-to-all | bytes 262144 | tf_op jit(solution)/shard_map/all_to_all | solution.py:51
  120.4 12.9 %all-gather.1 = bf16[256,128]{1,0:T(8,128)(2,1)} all-gather(bf16[64,128]{1,0:T(8,128)(2,1)S(1)} %reduce_sum.42), channel_id=3, replica_groups=mesh['dp_0'=4,'dp_1'=16,'mp'=8] {'dp_0'}, dimensions={0}, use_global_device_ids=true | all-gather | bytes 81920 | tf_op jit(solution)/shard_map/all_gather | solution.py:22
  133.3 0.0 all-gather.7.cloned.1.call-update
  134.0 65.6 %all-gather.7.cloned.1.call-done = bf16[64,64,128]{2,1,0:T(8,128)(2,1)} async-done(((bf16[4,64,128]{2,1,0:T(8,128)(2,1)}), bf16[64,64,128]{2,1,0:T(8,128)(2,1)}) %all-gather.7.cloned.1.call-update) | async-done | bytes 1048592 | tf_op jit(solution)/shard_map/all_gather | solution.py:22
  199.6 0.0 copy-start.1
  199.6 1.5 copy.21
  201.1 0.0 copy-done.2
  201.1 0.4 copy-done.1
  201.5 1.1 fusion.9
  (7 shorter events, 0.1 us)
Async XLA Ops:
  6.5 91.8 %copy-start = (bf16[8192,128]{1,0:T(8,128)(2,1)S(1)}, bf16[8192,128]{1,0:T(8,128)(2,1)}, u32[]{:S(2)}) copy-start(bf16[8192,128]{1,0:T(8,128)(2,1)} %param.11) | copy-start | bytes 6291460
  6.5 88.1 %all-gather.5.cloned.1.call-start = ((), (), s32[]{:S(2)}) async-start(), calls=%async_computation.2 | async-start | bytes 1114112 | tf_op jit(solution)/shard_map/all_gather | solution.py:22
  97.9 0.8 copy-start.3
  98.6 10.7 %copy-start.4 = (bf16[16,64,128]{2,1,0:T(8,128)(2,1)S(1)}, bf16[16,64,128]{2,1,0:T(8,128)(2,1)}, u32[]{:S(2)}) copy-start(bf16[16,64,128]{2,1,0:T(8,128)(2,1)} %param.14) | copy-start | bytes 786436
  99.9 9.4 %all-to-all-start = ((bf16[8,64,128]{2,1,0:T(8,128)(2,1)}), bf16[8,64,128]{2,1,0:T(8,128)(2,1)S(1)}, u32[]{:S(2)}, u32[]{:S(2)}) async-start(bf16[8,64,128]{2,1,0:T(8,128)(2,1)} %broadcast_in_dim.43), calls=%async_computation | async-start | bytes 262144 | tf_op jit(solution)/shard_map/all_to_all | solution.py:35
  104.7 95.0 %all-gather.7.cloned.1.call-start = ((), (), s32[]{:S(2)}) async-start(), calls=%async_computation.3 | async-start | bytes 1114112 | tf_op jit(solution)/shard_map/all_gather | solution.py:22
  109.3 1.3 copy-start.5
  111.8 89.3 %copy-start.2 = (bf16[64,128]{1,0:T(8,128)(2,1)S(1)}, bf16[64,128]{1,0:T(8,128)(2,1)}, u32[]{:S(2)}) copy-start(bf16[64,128]{1,0:T(8,128)(2,1)} %param.9) | copy-start | bytes 49156
  199.6 1.9 copy-start.1
Sparse Core Ops, SparseCore 0:
  20.7 73.8 all-gather.4
  133.4 66.1 all-gather.6
where the time goes:
time: 210 us
  waiting for transfers between devices  140 us (67%)
  blocking collectives  35.5 us (17%)
  between operations  14.2 us (7%)
  local copies, waits for them, and re-layouts  7.49 us (4%)
  starting transfers between devices  4.81 us (2%)
  other arithmetic  4.52 us (2%)
  matrix products  3.47 us (2%)
    all_gather x2, waiting for transfers between devices, gather_in_order(): parts = lax.all_gather(parts, axes[k], axis=0, tiled=True)  135 us
    all_gather x2, blocking collectives, gather_in_order(): parts = lax.all_gather(parts, axes[k], axis=0, tiled=True)  27 us
    all_to_all x1, blocking collectives, sent_and_summed(): parts = lax.all_to_all(split_up(value, dim, peers), axis, 0, 0, tiled=True)  8.49 us
    all_to_all x1, starting transfers between devices, from_everyone(): return lax.all_to_all(copies, axis, split_axis=0, concat_axis=0, tiled=True)  4.8 us
    all_to_all x1, waiting for transfers between devices, from_everyone(): return lax.all_to_all(copies, axis, split_axis=0, concat_axis=0, tiled=True)  4.26 us
  transfers between devices with their start and end apart: 3, of which 3 were waited for; matrix products, arithmetic and copies ran while one was open for 2% of the time, Pallas kernels for 0%

commit v1 on v0

v1 whole, which is shorter than its diff:
```python
import jax
import jax.numpy as jnp
from jax import lax
from jax.experimental import pallas as pl
from jax.experimental.pallas import tpu as pltpu
from jax.sharding import PartitionSpec as P

MESH = pl.DeviceIdType.MESH
NY, NZ, NX = 4, 16, 4
ND = NY * NZ
ROWS = 64
DH = 128
VT = 64
OWN = 16
IMAGES = 128
HALF = ROWS // 2
EPS = 1e-05
F32 = jnp.float32
BF16 = jnp.bfloat16


def kernel(
    tok_h, gain_h, wq_h, wo_h, gate_s, key_h, val_h, act_s, slot_s,
    out_ref,
    tbuf, abuf, wq, wo, gain, kbuf, vbuf, qf, of,
    local_sem, t_send, t_recv, a_send, a_recv, kv_send, kv_recv,
):
    dp = lax.axis_index("dp")
    mp = lax.axis_index("mp")
    y, z = dp // NZ, lax.rem(dp, NZ)
    x, core = mp // 2, lax.rem(mp, 2)
    ys = [lax.rem(y + d, NY) for d in range(NY)]
    zs = [lax.rem(z + d, NZ) for d in range(NZ)]
    xs = [lax.rem(x + d, NX) for d in range(NX)]

    def block(dy, dz):
        return ys[dy % NY] * NZ + zs[dz % NZ]

    def plane_peer(py, pz):
        return (block(py, pz), mp)

    def line_peer(px):
        return (dp, xs[px % NX] * 2 + core)

    sibling = (dp, x * 2 + (1 - core))

    locals_ = [
        pltpu.make_async_copy(tok_h, tbuf.at[dp], local_sem.at[0]),
        pltpu.make_async_copy(gain_h, gain, local_sem.at[1]),
        pltpu.make_async_copy(wq_h, wq, local_sem.at[2]),
        pltpu.make_async_copy(wo_h, wo, local_sem.at[3]),
        pltpu.make_async_copy(key_h, kbuf.at[pl.ds(mp * OWN, OWN)], local_sem.at[4]),
        pltpu.make_async_copy(val_h, vbuf.at[pl.ds(mp * OWN, OWN)], local_sem.at[5]),
    ]
    for copy in locals_:
        copy.start()

    barrier = pltpu.get_barrier_semaphore()
    partners = [plane_peer(0, d) for d in (1, -1, 2, -2, 5, -5)]
    partners += [plane_peer(d, 0) for d in (1, -1)]
    partners += [line_peer(1), line_peer(-1), sibling]
    for peer in partners:
        pl.semaphore_signal(barrier, inc=1, device_id=peer, device_id_type=MESH)
    pl.semaphore_wait(barrier, len(partners))

    kv = ((kbuf, key_h, 0), (vbuf, val_h, 1))

    def images(px, same, part=None):
        owner = xs[px % NX] * 2 + (core if same else 1 - core)
        first, count = owner * OWN, OWN
        if part is not None:
            count = OWN // 2
            first = first + part * count
        return pl.ds(pl.multiple_of(first, count), count)

    def kv_copy(which, source, where, peer, sem):
        buf, _, n = kv[which]
        return pltpu.make_async_remote_copy(
            src_ref=source, dst_ref=buf.at[where], send_sem=kv_send.at[n],
            recv_sem=kv_recv.at[n, sem], device_id=peer, device_id_type=MESH)

    def kv_own(which):
        source = kv[which][1]
        where = images(0, True)
        kv_copy(which, source, where, line_peer(1), 0).start()
        kv_copy(which, source, where, line_peer(-1), 1).start()
        kv_copy(which, source, where, sibling, 4).start()

    def kv_wait(which, where, sem):
        buf = kv[which][0]
        kv_copy(which, buf.at[where], where, sibling, sem).wait_recv()

    def kv_pass(which):
        buf = kv[which][0]
        for px, sem, part in ((-1, 0, 0), (1, 1, 1)):
            where = images(px, True)
            kv_wait(which, where, sem)
            half = images(px, True, part)
            kv_copy(which, buf.at[half], half, line_peer(-px), 2 + part).start()
            kv_copy(which, buf.at[where], where, sibling, 5 + sem).start()

    def kv_pass_half(which):
        buf = kv[which][0]
        for part in (0, 1):
            half = images(2, True, part)
            kv_wait(which, half, 2 + part)
            kv_copy(which, buf.at[half], half, sibling, 7 + part).start()

    def kv_finish(which):
        kv_wait(which, images(0, False), 4)
        kv_wait(which, images(-1, False), 5)
        kv_wait(which, images(1, False), 6)
        kv_wait(which, images(2, False, 0), 7)
        kv_wait(which, images(2, False, 1), 8)

    def gather(buf, send_sem, recv_sem):
        def copy(dy, dz, py, pz, part=None):
            place = buf.at[block(dy, dz)]
            sem = ((dy - py) % NY) * NZ + (dz - pz) % NZ
            if part is not None:
                place = place.at[pl.ds(part * HALF, HALF)]
                sem = sem if part == 0 else ND
            return pltpu.make_async_remote_copy(
                src_ref=place, dst_ref=place, send_sem=send_sem,
                recv_sem=recv_sem.at[sem], device_id=plane_peer(py, pz), device_id_type=MESH)

        def wait(dy, dz):
            if dy % NY == 0 and dz % NZ == 8:
                copy(0, 7, 0, -1, 0).wait_recv()
                part = buf.at[block(0, 8)].at[pl.ds(HALF, HALF)]
                pltpu.make_async_remote_copy(
                    src_ref=part, dst_ref=part, send_sem=send_sem, recv_sem=recv_sem.at[ND],
                    device_id=plane_peer(0, 1), device_id_type=MESH).wait_recv()
                return
            place = buf.at[block(dy, dz)]
            pltpu.make_async_remote_copy(
                src_ref=place, dst_ref=place, send_sem=send_sem,
                recv_sem=recv_sem.at[(dy % NY) * NZ + dz % NZ],
                device_id=plane_peer(0, 1), device_id_type=MESH).wait_recv()

        def along_y(dz):
            copy(0, dz, 1, 0).start()
            copy(0, dz, -1, 0).start()

        def own():
            for pz in (5, -5, 1, -1, 2, -2):
                copy(0, 0, 0, pz).start()
            along_y(0)

        def line(*offsets):
            for dz in offsets:
                wait(0, dz)
                if dz in (5, -5):
                    for pz in (1, -1, 2, -2):
                        copy(0, dz, 0, pz).start()
                if dz == 7:
                    copy(0, dz, 0, -1, 0).start()
                if dz == -7:
                    copy(0, dz, 0, 1, 1).start()
                along_y(dz)

        def relay(*offsets):
            for dz in offsets:
                for dy in (1, -1):
                    wait(dy, dz)
                    if (dz % 2 == 0) == (dy == 1):
                        copy(dy, dz, -dy, 0).start()

        def last():
            for dz in range(NZ):
                wait(2, dz)

        def sent():
            whole = buf.at[pl.ds(0, ND - 1)]
            pltpu.make_async_copy(whole, whole, send_sem).wait()

        return own, line, relay, last, sent

    own, line, relay, last, t_sent = gather(tbuf, t_send.at[0], t_recv)
    locals_[0].wait()
    own()
    kv_own(0)
    kv_own(1)
    line(1, -1)
    relay(0)
    line(2, -2)
    relay(1, -1)
    line(5, -5)
    relay(2, -2)
    line(4, -4, 6, -6)
    relay(5, -5)
    line(3, -3, 7, -7)
    kv_pass(0)
    relay(4, -4, 6, -6)
    line(8)
    relay(3, -3, 7, -7)
    relay(8)
    kv_pass(1)
    last()

    def add_row(d, total):
        return total + tbuf[d].astype(F32)

    total = lax.fori_loop(0, ND, add_row, jnp.zeros((ROWS, DH), F32), unroll=8)
    mean = jnp.sum(total, axis=1, keepdims=True) * (1.0 / (ND * DH))
    mean_b = jnp.broadcast_to(mean, (ROWS, DH))

    def add_square(d, total):
        c = tbuf[d].astype(F32) - mean_b
        return total + c * c

    square = lax.fori_loop(0, ND, add_square, jnp.zeros((ROWS, DH), F32), unroll=8)
    variance = jnp.sum(square, axis=1, keepdims=True) * (1.0 / (ND * DH))
    scale_b = jnp.broadcast_to(lax.rsqrt(variance + EPS), (ROWS, DH))
    locals_[1].wait()
    locals_[2].wait()

    def project(i, acc):
        parts = []
        for j in range(4):
            d = i * 4 + j
            g = gain[pl.ds(d, 1), :]
            parts.append((((tbuf[d].astype(F32) - mean_b) * scale_b) * g).astype(BF16))
        lhs = jnp.concatenate(parts, axis=1)
        rhs = wq[pl.ds(pl.multiple_of(i * 4 * DH, 4 * DH), 4 * DH), :]
        return acc + jnp.dot(lhs, rhs, preferred_element_type=F32)

    queries = lax.fori_loop(0, ND // 4, project, jnp.zeros((ROWS, DH), F32), unroll=4)
    qf[...] = queries.astype(BF16).astype(F32)

    kv_pass_half(0)
    kv_pass_half(1)
    locals_[4].wait()
    locals_[5].wait()
    kv_finish(0)
    kv_finish(1)

    def attend(i, carry):
        outs = []
        for j in range(8):
            image = act_s[j % 4, mp * (ROWS // 4) + i * 2 + j // 4]
            slot = slot_s[image]
            q = qf[pl.ds(i * 8 + j, 1), :]
            s = jnp.sum(kbuf[slot].astype(F32) * q, axis=1, keepdims=True) * (DH ** -0.5)
            e = jnp.exp(s - jnp.max(s, axis=0, keepdims=True))
            p = (e / jnp.sum(e, axis=0, keepdims=True)).astype(BF16).astype(F32)
            outs.append(jnp.sum(p * vbuf[slot].astype(F32), axis=0, keepdims=True))
        of[pl.ds(pl.multiple_of(i * 8, 8), 8), :] = jnp.concatenate(outs, axis=0)
        return carry

    lax.fori_loop(0, ROWS // 8, attend, 0)
    abuf[dp] = of[...].astype(BF16)

    own, line, relay, last, a_sent = gather(abuf, a_send.at[0], a_recv)
    own()
    line(1, -1)
    relay(0)
    line(2, -2)
    relay(1, -1)
    line(5, -5)
    relay(2, -2)
    line(4, -4, 6, -6)
    relay(5, -5)
    line(3, -3, 7, -7)
    relay(4, -4, 6, -6)
    line(8)
    relay(3, -3, 7, -7)
    relay(8)
    last()

    locals_[3].wait()

    def project_out(i, acc):
        lhs = jnp.concatenate([abuf[i * 4 + j] for j in range(4)], axis=1)
        rhs = wo[pl.ds(pl.multiple_of(i * 4 * DH, 4 * DH), 4 * DH), :]
        return acc + jnp.dot(lhs, rhs, preferred_element_type=F32)

    projected = lax.fori_loop(0, ND // 4, project_out, jnp.zeros((ROWS, DH), F32), unroll=4)
    gate = jnp.tanh(jnp.full((ROWS, DH), gate_s[0], F32))
    out_ref[...] = (tbuf[dp].astype(F32) + gate * projected).astype(BF16)

    t_sent()
    a_sent()
    for which in (0, 1):
        whole = kv[which][0].at[pl.ds(0, 7 * OWN)]
        pltpu.make_async_copy(whole, whole, kv_send.at[which]).wait()


def body(tokens, norm_gain, query_weight, out_weight, gate_scalar, image_keys, image_values, active_image, image_slot):
    hbm = pl.BlockSpec(memory_space=pltpu.HBM)
    smem = pl.BlockSpec(memory_space=pltpu.SMEM)
    vmem = pl.BlockSpec(memory_space=pltpu.VMEM)
    dma = pltpu.SemaphoreType.DMA
    return pl.pallas_call(
        kernel,
        out_shape=jax.ShapeDtypeStruct((ROWS, DH), BF16),
        in_specs=[hbm, hbm, hbm, hbm, smem, hbm, hbm, smem, smem],
        out_specs=vmem,
        scratch_shapes=[
            pltpu.VMEM((ND, ROWS, DH), BF16),
            pltpu.VMEM((ND, ROWS, DH), BF16),
            pltpu.VMEM((ND * DH, DH), BF16),
            pltpu.VMEM((ND * DH, DH), BF16),
            pltpu.VMEM((ND, DH), F32),
            pltpu.VMEM((IMAGES, VT, DH), BF16),
            pltpu.VMEM((IMAGES, VT, DH), BF16),
            pltpu.VMEM((ROWS, DH), F32),
            pltpu.VMEM((ROWS, DH), F32),
            dma((6,)),
            dma((1,)),
            dma((ND + 1,)),
            dma((1,)),
            dma((ND + 1,)),
            dma((2,)),
            dma((2, 9)),
        ],
        compiler_params=pltpu.CompilerParams(
            collective_id=0, has_side_effects=True, vmem_limit_bytes=56 * 1024 * 1024
        ),
        name="gated_cross_attention",
    )(tokens, norm_gain.reshape(ND, DH), query_weight, out_weight, gate_scalar,
      image_keys, image_values, active_image.T, image_slot)


def solution(mesh):
    placed = (
        P("mp", "dp"),
        P(),
        P(None, "dp"),
        P(None, "dp"),
        P(),
        P("mp", None, "dp"),
        P("mp", None, "dp"),
        P(),
        P(),
    )
    return jax.shard_map(body, mesh=mesh, in_specs=placed, out_specs=P("mp", "dp"), check_vma=False)
```

time: 210 us -> 67.3 us (0.32)
  the two profiles are of different devices: /device:TPU:2 before, /device:TPU:1 now
where the time goes in v1:
time: 67.3 us; the launch traced here: 66.5 us
  Pallas kernels  64.5 us (96%)
  local copies, waits for them, and re-layouts  1.32 us (2%)
    pallas_call x1, Pallas kernels, body(): pl.pallas_call(kernel, out_shape=jax.ShapeDtypeStruct((ROWS, DH), BF16),...  64.5 us

profile of v1, /device:TPU:1, one launch (start us, length us, event | category | flops | bytes accessed | tf_op | source)
XLA Modules:
  0.0 66.5 jit_solution(2606337787219626592)
XLA Ops:
  0.7 64.5 %gated_cross_attention.1 = bf16[64,128]{1,0:T(8,128)(2,1)} custom-call(bf16[64,128]{1,0:T(8,128)(2,1)} %tok_h.1, f32[64,128]{1,0:T(8,128)} %bitcast.2, bf16[8192,128]{1,0:T(8,128)(2,1)} %wq_h.1, bf16[8192,128]{1,0:T(8,128)(2,1)} %wo_h.1, f32[1]{0:T(128)S(6)} %copy.11.gate_s, bf16[16,64,128]{2,1,0:T(8,128)(2,1)} %key_h.1, bf16[16,64,128]{2,1,0:T(8,128)(2,1)} %val_h.1, ...), custom_call_target="tpu_custom_call" | custom-call | tf_op jit(solution)/shard_map/gated_cross_attention/pallas_call | solution.py:294
  65.2 1.3 %copy.12 = bf16[64,128]{1,0:T(8,128)(2,1)} copy(bf16[64,128]{1,0:T(8,128)(2,1)} %gated_cross_attention.1) | data formatting | bytes 32768

commit v2 on v1

v2 whole, which is shorter than its diff:
```python
import jax
import jax.numpy as jnp
from jax import lax
from jax.experimental import pallas as pl
from jax.experimental.pallas import tpu as pltpu
from jax.sharding import PartitionSpec as P

MESH = pl.DeviceIdType.MESH
NY, NZ, NX = 4, 16, 4
ND = NY * NZ
ROWS = 64
DH = 128
VT = 64
OWN = 16
HALF = OWN // 2
IMAGES = 128
EPS = 1e-05
F32 = jnp.float32
BF16 = jnp.bfloat16

SPREAD = (
    ((0, 0), ((0, 5), (3, 0), (2, 0), (0, 12), (0, 1), (0, 15))),
    ((3, 0), ((3, 2), (3, 14), (1, 0))),
    ((0, 1), ((0, 4), (3, 1), (1, 1), (2, 1))),
    ((0, 15), ((2, 15), (1, 15), (3, 15))),
    ((2, 0), ((2, 14),)),
    ((0, 12), ((1, 12), (0, 9), (3, 12), (2, 12), (0, 10), (0, 13))),
    ((0, 5), ((0, 6), (2, 5), (1, 5), (3, 5), (0, 8))),
    ((3, 1), ()),
    ((1, 1), ()),
    ((3, 2), ((1, 2), (3, 3), (0, 2), (2, 2))),
    ((3, 14), ((3, 13),)),
    ((3, 15), ()),
    ((1, 15), ()),
    ((2, 14), ((2, 13), (1, 14))),
    ((1, 0), ()),
    ((2, 1), ()),
    ((0, 4), ((2, 4), (0, 3), (1, 4), (3, 4))),
    ((2, 15), ()),
    ((1, 12), ((1, 13), (1, 11))),
    ((3, 12), ((3, 11), (3, 10))),
    ((0, 13), ((0, 14),)),
    ((0, 6), ((2, 6), (3, 6), (1, 6))),
    ((1, 5), ((1, 7),)),
    ((3, 5), ((3, 7),)),
    ((2, 12), ((2, 11),)),
    ((0, 10), ((2, 10), (1, 10), (0, 11))),
    ((2, 5), ((2, 3), (2, 7))),
    ((0, 9), ((3, 9), (2, 9), (1, 9))),
    ((0, 2), ()),
    ((2, 2), ()),
    ((3, 3), ()),
    ((3, 13), ()),
    ((0, 8), ((2, 8), (1, 8), (0, 7), (3, 8))),
    ((1, 2), ()),
    ((2, 13), ()),
    ((1, 14), ()),
    ((0, 3), ()),
    ((1, 4), ((1, 3),)),
    ((1, 13), ()),
    ((3, 4), ()),
    ((1, 11), ()),
    ((2, 4), ()),
    ((0, 14), ()),
    ((3, 11), ()),
    ((1, 6), ()),
    ((3, 6), ()),
    ((2, 11), ()),
    ((2, 6), ()),
    ((0, 11), ()),
    ((1, 10), ()),
    ((3, 9), ()),
    ((3, 10), ()),
    ((1, 9), ()),
    ((2, 10), ()),
    ((1, 7), ()),
    ((2, 3), ()),
    ((3, 8), ()),
    ((3, 7), ()),
    ((0, 7), ()),
    ((1, 8), ()),
    ((2, 9), ()),
    ((2, 7), ()),
    ((2, 8), ()),
    ((1, 3), ()),
)


def kernel(
    tok_h, gain_h, wq_h, wo_h, gate_s, key_h, val_h, act_s, slot_s,
    out_ref,
    tbuf, abuf, wq, wo, gain, kbuf, vbuf, qf, of, pbuf,
    local_sem, t_send, t_recv, a_send, a_recv, kv_send, kv_recv,
):
    dp = lax.axis_index("dp")
    mp = lax.axis_index("mp")
    y, z = dp // NZ, lax.rem(dp, NZ)
    x, core = mp // 2, lax.rem(mp, 2)
    ys = [lax.rem(y + d, NY) * NZ for d in range(NY)]
    zs = [lax.rem(z + d, NZ) for d in range(NZ)]
    xs = [lax.rem(x + d, NX) * 2 for d in range(NX)]

    def block(dy, dz):
        return ys[dy % NY] + zs[dz % NZ]

    def plane_peer(dy, dz):
        return (block(dy, dz), mp)

    def line_peer(px):
        return (dp, xs[px % NX] + core)

    sibling = (dp, xs[0] + (1 - core))

    local = [
        pltpu.make_async_copy(src, dst, local_sem.at[i])
        for i, (src, dst) in enumerate((
            (tok_h, tbuf.at[dp]),
            (gain_h, gain),
            (wq_h, wq),
            (wo_h, wo),
            (key_h, kbuf.at[pl.ds(mp * OWN, OWN)]),
            (val_h, vbuf.at[pl.ds(mp * OWN, OWN)]),
        ))
    ]
    for copy in local:
        copy.start()

    barrier = pltpu.get_barrier_semaphore()
    steps = {((c[0] - p[0]) % NY, (c[1] - p[1]) % NZ) for p, onward in SPREAD for c in onward}
    steps |= {((-a) % NY, (-b) % NZ) for a, b in steps}
    partners = [plane_peer(*step) for step in sorted(steps)]
    partners += [line_peer(1), line_peer(-1), sibling]
    for peer in partners:
        pl.semaphore_signal(barrier, inc=1, device_id=peer, device_id_type=MESH)
    pl.semaphore_wait(barrier, len(partners))

    kv = ((kbuf, key_h), (vbuf, val_h))

    def images(px, same, part=None):
        first = (xs[px % NX] + (core if same else 1 - core)) * OWN
        if part is None:
            return pl.ds(pl.multiple_of(first, OWN), OWN)
        return pl.ds(pl.multiple_of(first + part * HALF, HALF), HALF)

    def kv_copy(which, source, where, peer, sem):
        return pltpu.make_async_remote_copy(
            src_ref=source, dst_ref=kv[which][0].at[where], send_sem=kv_send.at[which],
            recv_sem=kv_recv.at[which, sem], device_id=peer, device_id_type=MESH)

    ARRIVED = ((-1, 0), (-1, 1), (1, 0), (1, 1), (2, 0), (2, 1))

    def kv_own_half(which, px, part):
        source = kv[which][1].at[pl.ds(part * HALF, HALF)]
        kv_copy(which, source, images(0, True, part), line_peer(px), (0 if px == 1 else 2) + part).start()

    def kv_own_sibling(which):
        kv_copy(which, kv[which][1], images(0, True), sibling, 6).start()

    def kv_wait(which, where, sem):
        kv_copy(which, kv[which][0].at[where], where, sibling, sem).wait_recv()

    def kv_arrive(which, sem, onward=None):
        px, part = ARRIVED[sem]
        where = images(px, True, part)
        kv_wait(which, where, sem)
        source = kv[which][0].at[where]
        if onward is not None:
            kv_copy(which, source, where, line_peer(onward), 4 + part).start()
        kv_copy(which, source, where, sibling, 7 + sem).start()

    def kv_finish(which):
        kv_wait(which, images(0, False), 6)
        for sem, (px, part) in enumerate(ARRIVED):
            kv_wait(which, images(px, False, part), 7 + sem)

    index_of = {place: i for i, (place, _) in enumerate(SPREAD)}

    def arrived_block(place):
        return block(-place[0], -place[1])

    def spread(buf, send_sem, recv_sem, i):
        place, onward = SPREAD[i]
        here = buf.at[arrived_block(place)]
        if i > 0:
            pltpu.make_async_remote_copy(
                src_ref=here, dst_ref=here, send_sem=send_sem, recv_sem=recv_sem.at[i],
                device_id=sibling, device_id_type=MESH).wait_recv()
        for target in onward:
            pltpu.make_async_remote_copy(
                src_ref=here, dst_ref=here, send_sem=send_sem, recv_sem=recv_sem.at[index_of[target]],
                device_id=plane_peer(target[0] - place[0], target[1] - place[1]),
                device_id_type=MESH).start()

    def all_sent(buf, send_sem):
        whole = buf.at[pl.ds(0, ND - 1)]
        pltpu.make_async_copy(whole, whole, send_sem).wait()

    local[0].wait()
    spread(tbuf, t_send.at[0], t_recv, 0)
    for which, parts in ((0, (0, 1)), (1, (0,))):
        for part in parts:
            kv_own_half(which, 1, part)
            kv_own_half(which, -1, 1 - part)
        kv_own_sibling(which)

    own = tbuf[dp].astype(F32)
    shift = jnp.broadcast_to(jnp.sum(own, axis=1, keepdims=True) * (1.0 / DH), (ROWS, DH))
    total = own - shift
    square = total * total
    kv_steps = {
        7: ((0, 0, 1), (0, 3, -1)),
        24: ((0, 1, None), (0, 2, None)),
        46: ((1, 0, 1), (1, 3, -1)),
        63: ((0, 4, None), (0, 5, None)),
    }
    for i in range(1, ND):
        spread(tbuf, t_send.at[0], t_recv, i)
        part = tbuf[arrived_block(SPREAD[i][0])].astype(F32) - shift
        total = total + part
        square = square + part * part
        for which, sem, onward in kv_steps.get(i, ()):
            kv_arrive(which, sem, onward)
        if i == 7:
            kv_own_half(1, 1, 1)
            kv_own_half(1, -1, 0)

    drift = jnp.sum(total, axis=1, keepdims=True) * (1.0 / (ND * DH))
    variance = jnp.sum(square, axis=1, keepdims=True) * (1.0 / (ND * DH)) - drift * drift
    mean_b = shift + drift
    scale_b = jnp.broadcast_to(lax.rsqrt(jnp.maximum(variance, 0.0) + EPS), (ROWS, DH))
    local[1].wait()
    local[2].wait()

    def project(i, acc):
        parts = []
        for j in range(4):
            d = i * 4 + j
            g = gain[pl.ds(d, 1), :]
            parts.append((((tbuf[d].astype(F32) - mean_b) * scale_b) * g).astype(BF16))
        lhs = jnp.concatenate(parts, axis=1)
        rhs = wq[pl.ds(pl.multiple_of(i * 4 * DH, 4 * DH), 4 * DH), :]
        return acc + jnp.dot(lhs, rhs, preferred_element_type=F32)

    queries = lax.fori_loop(0, ND // 4, project, jnp.zeros((ROWS, DH), F32), unroll=4)
    qf[...] = queries.astype(BF16).astype(F32)

    kv_arrive(1, 1)
    kv_arrive(1, 2)
    local[4].wait()
    kv_finish(0)

    def slot_of(i, j):
        image = act_s[j % 4, mp * (ROWS // 4) + i * 2 + j // 4]
        return slot_s[image]

    def weigh(i, carry):
        for j in range(8):
            q = qf[pl.ds(i * 8 + j, 1), :]
            s = jnp.sum(kbuf[slot_of(i, j)].astype(F32) * q, axis=1, keepdims=True) * (DH ** -0.5)
            e = jnp.exp(s - jnp.max(s, axis=0, keepdims=True))
            p = (e / jnp.sum(e, axis=0, keepdims=True)).astype(BF16).astype(F32)
            pbuf[i * 8 + j] = jnp.broadcast_to(p, (VT, DH))
        return carry

    lax.fori_loop(0, ROWS // 8, weigh, 0)

    kv_arrive(1, 4)
    kv_arrive(1, 5)
    local[5].wait()
    kv_finish(1)

    def collect(i, carry):
        outs = [
            jnp.sum(pbuf[i * 8 + j] * vbuf[slot_of(i, j)].astype(F32), axis=0, keepdims=True)
            for j in range(8)
        ]
        of[pl.ds(pl.multiple_of(i * 8, 8), 8), :] = jnp.concatenate(outs, axis=0)
        return carry

    lax.fori_loop(0, ROWS // 8, collect, 0)
    abuf[dp] = of[...].astype(BF16)

    final = max(i for i, (_, onward) in enumerate(SPREAD) if onward) + 1
    for i in range(final):
        spread(abuf, a_send.at[0], a_recv, i)
    local[3].wait()

    def project_out(acc, first, last):
        places = [arrived_block(SPREAD[i][0]) for i in range(first, last)]
        lhs = jnp.concatenate([abuf[b] for b in places], axis=1)
        rhs = jnp.concatenate([wo[pl.ds(pl.multiple_of(b * DH, DH), DH), :] for b in places], axis=0)
        return acc + jnp.dot(lhs, rhs, preferred_element_type=F32)

    projected = jnp.zeros((ROWS, DH), F32)
    for first in range(0, final, 8):
        projected = project_out(projected, first, min(first + 8, final))
    for first in range(final, ND, 4):
        last = min(first + 4, ND)
        for i in range(first, last):
            spread(abuf, a_send.at[0], a_recv, i)
        projected = project_out(projected, first, last)
    gate = jnp.tanh(jnp.full((ROWS, DH), gate_s[0], F32))
    out_ref[...] = (tbuf[dp].astype(F32) + gate * projected).astype(BF16)

    all_sent(tbuf, t_send.at[0])
    all_sent(abuf, a_send.at[0])
    for which in (0, 1):
        whole = kv[which][0].at[pl.ds(0, 7 * OWN)]
        pltpu.make_async_copy(whole, whole, kv_send.at[which]).wait()


def body(tokens, norm_gain, query_weight, out_weight, gate_scalar, image_keys, image_values, active_image, image_slot):
    hbm = pl.BlockSpec(memory_space=pltpu.HBM)
    smem = pl.BlockSpec(memory_space=pltpu.SMEM)
    vmem = pl.BlockSpec(memory_space=pltpu.VMEM)
    dma = pltpu.SemaphoreType.DMA
    return pl.pallas_call(
        kernel,
        out_shape=jax.ShapeDtypeStruct((ROWS, DH), BF16),
        in_specs=[hbm, hbm, hbm, hbm, smem, hbm, hbm, smem, smem],
        out_specs=vmem,
        scratch_shapes=[
            pltpu.VMEM((ND, ROWS, DH), BF16),
            pltpu.VMEM((ND, ROWS, DH), BF16),
            pltpu.VMEM((ND * DH, DH), BF16),
            pltpu.VMEM((ND * DH, DH), BF16),
            pltpu.VMEM((ND, DH), F32),
            pltpu.VMEM((IMAGES, VT, DH), BF16),
            pltpu.VMEM((IMAGES, VT, DH), BF16),
            pltpu.VMEM((ROWS, DH), F32),
            pltpu.VMEM((ROWS, DH), F32),
            pltpu.VMEM((ROWS, VT, DH), F32),
            dma((6,)),
            dma((1,)),
            dma((ND,)),
            dma((1,)),
            dma((ND,)),
            dma((2,)),
            dma((2, 13)),
        ],
        compiler_params=pltpu.CompilerParams(
            collective_id=0, has_side_effects=True, vmem_limit_bytes=56 * 1024 * 1024
        ),
        name="gated_cross_attention",
    )(tokens, norm_gain.reshape(ND, DH), query_weight, out_weight, gate_scalar,
      image_keys, image_values, active_image.T, image_slot)


def solution(mesh):
    placed = (
        P("mp", "dp"),
        P(),
        P(None, "dp"),
        P(None, "dp"),
        P(),
        P("mp", None, "dp"),
        P("mp", None, "dp"),
        P(),
        P(),
    )
    return jax.shard_map(body, mesh=mesh, in_specs=placed, out_specs=P("mp", "dp"), check_vma=False)
```

time: 67.3 us -> 56.4 us (0.84)
  Pallas kernels: 64.5 us -> 54.2 us
    pallas_call x1, Pallas kernels: 64.5 us -> 54.2 us  [body(): pl.pallas_call(kernel, out_shape=jax.ShapeDtypeStruct((ROWS, DH), BF16),...]
where the time goes in v2:
time: 56.4 us; the launch traced here: 56.2 us
  Pallas kernels  54.2 us (96%)
  local copies, waits for them, and re-layouts  1.32 us (2%)
  between operations  0.66 us (1%)
    pallas_call x1, Pallas kernels, body(): pl.pallas_call(kernel, out_shape=jax.ShapeDtypeStruct((ROWS, DH), BF16),...  54.2 us
    unnamed x1, local copies, waits for them, and re-layouts  1.32 us

profile of v2, /device:TPU:1, one launch (start us, length us, event | category | flops | bytes accessed | tf_op | source)
XLA Modules:
  0.0 56.2 jit_solution(16978724046905273442)
XLA Ops:
  0.7 54.2 %gated_cross_attention.1 = bf16[64,128]{1,0:T(8,128)(2,1)} custom-call(bf16[64,128]{1,0:T(8,128)(2,1)} %tok_h.1, f32[64,128]{1,0:T(8,128)} %bitcast.2, bf16[8192,128]{1,0:T(8,128)(2,1)} %wq_h.1, bf16[8192,128]{1,0:T(8,128)(2,1)} %wo_h.1, f32[1]{0:T(128)S(6)} %copy.11.gate_s, bf16[16,64,128]{2,1,0:T(8,128)(2,1)} %key_h.1, bf16[16,64,128]{2,1,0:T(8,128)(2,1)} %val_h.1, ...), custom_call_target="tpu_custom_call" | custom-call | tf_op jit(solution)/shard_map/gated_cross_attention/pallas_call | solution.py:317
  54.9 1.3 %copy.12 = bf16[64,128]{1,0:T(8,128)(2,1)} copy(bf16[64,128]{1,0:T(8,128)(2,1)} %gated_cross_attention.1) | data formatting | bytes 32768

commit v3 on v2

--- a/solution.py
+++ b/solution.py
@@ -19,77 +19,77 @@
 BF16 = jnp.bfloat16
 
 SPREAD = (
-    ((0, 0), ((0, 5), (3, 0), (2, 0), (0, 12), (0, 1), (0, 15))),
-    ((3, 0), ((3, 2), (3, 14), (1, 0))),
-    ((0, 1), ((0, 4), (3, 1), (1, 1), (2, 1))),
-    ((0, 15), ((2, 15), (1, 15), (3, 15))),
-    ((2, 0), ((2, 14),)),
-    ((0, 12), ((1, 12), (0, 9), (3, 12), (2, 12), (0, 10), (0, 13))),
-    ((0, 5), ((0, 6), (2, 5), (1, 5), (3, 5), (0, 8))),
-    ((3, 1), ()),
+    ((0, 0), ((0, 5), (0, 11), (1, 0), (0, 15), (3, 0), (2, 0), (0, 3))),
+    ((1, 0), ((1, 1),)),
+    ((3, 0), ((3, 13), (3, 1))),
+    ((0, 15), ((0, 1), (2, 15), (1, 15), (0, 13), (0, 14), (3, 15))),
+    ((2, 0), ((2, 2),)),
+    ((0, 3), ((2, 3), (0, 4), (3, 3), (0, 2), (1, 3))),
+    ((0, 11), ((1, 11), (0, 8), (3, 11), (0, 10), (2, 11))),
+    ((0, 5), ((0, 7), (1, 5), (3, 5), (2, 5), (0, 6))),
     ((1, 1), ()),
-    ((3, 2), ((1, 2), (3, 3), (0, 2), (2, 2))),
-    ((3, 14), ((3, 13),)),
+    ((3, 1), ((2, 1),)),
+    ((1, 15), ()),
     ((3, 15), ()),
-    ((1, 15), ()),
-    ((2, 14), ((2, 13), (1, 14))),
-    ((1, 0), ()),
+    ((0, 14), ((1, 14), (3, 14))),
+    ((2, 15), ((2, 14),)),
+    ((0, 13), ((0, 12), (1, 13))),
+    ((0, 1), ()),
+    ((3, 13), ((2, 13),)),
+    ((3, 3), ()),
+    ((1, 3), ((1, 4), (1, 2))),
+    ((0, 4), ((3, 4), (2, 4))),
+    ((0, 2), ()),
+    ((2, 2), ((3, 2),)),
+    ((2, 3), ()),
+    ((1, 11), ((1, 9), (1, 12))),
+    ((3, 11), ((3, 9), (3, 12))),
+    ((0, 10), ((1, 10), (3, 10))),
+    ((1, 5), ((1, 6),)),
+    ((0, 6), ((3, 6),)),
+    ((3, 5), ()),
+    ((0, 7), ((1, 7), (2, 7), (3, 7))),
+    ((2, 11), ((2, 9), (2, 10), (2, 12))),
     ((2, 1), ()),
-    ((0, 4), ((2, 4), (0, 3), (1, 4), (3, 4))),
-    ((2, 15), ()),
-    ((1, 12), ((1, 13), (1, 11))),
-    ((3, 12), ((3, 11), (3, 10))),
-    ((0, 13), ((0, 14),)),
-    ((0, 6), ((2, 6), (3, 6), (1, 6))),
-    ((1, 5), ((1, 7),)),
-    ((3, 5), ((3, 7),)),
-    ((2, 12), ((2, 11),)),
-    ((0, 10), ((2, 10), (1, 10), (0, 11))),
-    ((2, 5), ((2, 3), (2, 7))),
-    ((0, 9), ((3, 9), (2, 9), (1, 9))),
-    ((0, 2), ()),
-    ((2, 2), ()),
-    ((3, 3), ()),
-    ((3, 13), ()),
-    ((0, 8), ((2, 8), (1, 8), (0, 7), (3, 8))),
+    ((1, 14), ()),
+    ((0, 8), ((2, 8), (1, 8), (0, 9), (3, 8))),
+    ((2, 5), ((2, 6),)),
+    ((3, 14), ()),
+    ((2, 14), ()),
+    ((1, 13), ()),
+    ((0, 12), ()),
+    ((2, 13), ()),
+    ((1, 4), ()),
     ((1, 2), ()),
-    ((2, 13), ()),
-    ((1, 14), ()),
-    ((0, 3), ()),
-    ((1, 4), ((1, 3),)),
-    ((1, 13), ()),
     ((3, 4), ()),
-    ((1, 11), ()),
+    ((3, 2), ()),
+    ((1, 12), ()),
     ((2, 4), ()),
-    ((0, 14), ()),
-    ((3, 11), ()),
+    ((3, 12), ()),
+    ((1, 10), ()),
+    ((3, 10), ()),
+    ((1, 9), ()),
     ((1, 6), ()),
     ((3, 6), ()),
-    ((2, 11), ()),
+    ((1, 7), ()),
+    ((3, 9), ()),
+    ((2, 12), ()),
+    ((3, 7), ()),
+    ((0, 9), ()),
+    ((1, 8), ()),
+    ((2, 10), ()),
     ((2, 6), ()),
-    ((0, 11), ()),
-    ((1, 10), ()),
-    ((3, 9), ()),
-    ((3, 10), ()),
-    ((1, 9), ()),
-    ((2, 10), ()),
-    ((1, 7), ()),
-    ((2, 3), ()),
     ((3, 8), ()),
-    ((3, 7), ()),
-    ((0, 7), ()),
-    ((1, 8), ()),
-    ((2, 9), ()),
     ((2, 7), ()),
     ((2, 8), ()),
-    ((1, 3), ()),
+    ((2, 9), ()),
 )
 
 
 def kernel(
-    tok_h, gain_h, wq_h, wo_h, gate_s, key_h, val_h, act_s, slot_s,
+    tok_h, gain_h, wq_h, wo_h, gate_h, key_h, val_h, act_h, slot_h,
     out_ref,
-    tbuf, abuf, wq, wo, gain, kbuf, vbuf, qf, of, pbuf,
+    tbuf, abuf, wq, wo, gain, kbuf, vbuf, qf, of, pbuf, gate_s, act_s, slot_s,
     local_sem, t_send, t_recv, a_send, a_recv, kv_send, kv_recv,
 ):
     dp = lax.axis_index("dp")
@@ -120,6 +120,9 @@
             (wo_h, wo),
             (key_h, kbuf.at[pl.ds(mp * OWN, OWN)]),
             (val_h, vbuf.at[pl.ds(mp * OWN, OWN)]),
+            (gate_h, gate_s),
+            (act_h, act_s),
+            (slot_h, slot_s),
         ))
     ]
     for copy in local:
@@ -208,8 +211,8 @@
     total = own - shift
     square = total * total
     kv_steps = {
-        7: ((0, 0, 1), (0, 3, -1)),
-        24: ((0, 1, None), (0, 2, None)),
+        8: ((0, 0, 1), (0, 3, -1)),
+        26: ((0, 1, None), (0, 2, None)),
         46: ((1, 0, 1), (1, 3, -1)),
         63: ((0, 4, None), (0, 5, None)),
     }
@@ -220,7 +223,7 @@
         square = square + part * part
         for which, sem, onward in kv_steps.get(i, ()):
             kv_arrive(which, sem, onward)
-        if i == 7:
+        if i == 8:
             kv_own_half(1, 1, 1)
             kv_own_half(1, -1, 0)
 
@@ -246,7 +249,8 @@
 
     kv_arrive(1, 1)
     kv_arrive(1, 2)
-    local[4].wait()
+    for i in (4, 7, 8):
+        local[i].wait()
     kv_finish(0)
 
     def slot_of(i, j):
@@ -299,6 +303,7 @@
         for i in range(first, last):
             spread(abuf, a_send.at[0], a_recv, i)
         projected = project_out(projected, first, last)
+    local[6].wait()
     gate = jnp.tanh(jnp.full((ROWS, DH), gate_s[0], F32))
     out_ref[...] = (tbuf[dp].astype(F32) + gate * projected).astype(BF16)
 
@@ -311,13 +316,12 @@
 
 def body(tokens, norm_gain, query_weight, out_weight, gate_scalar, image_keys, image_values, active_image, image_slot):
     hbm = pl.BlockSpec(memory_space=pltpu.HBM)
-    smem = pl.BlockSpec(memory_space=pltpu.SMEM)
     vmem = pl.BlockSpec(memory_space=pltpu.VMEM)
     dma = pltpu.SemaphoreType.DMA
     return pl.pallas_call(
         kernel,
-        out_shape=jax.ShapeDtypeStruct((ROWS, DH), BF16),
-        in_specs=[hbm, hbm, hbm, hbm, smem, hbm, hbm, smem, smem],
+        out_shape=pltpu.VMEM((ROWS, DH), BF16),
+        in_specs=[hbm] * 9,
         out_specs=vmem,
         scratch_shapes=[
             pltpu.VMEM((ND, ROWS, DH), BF16),
@@ -330,7 +334,10 @@
             pltpu.VMEM((ROWS, DH), F32),
             pltpu.VMEM((ROWS, DH), F32),
             pltpu.VMEM((ROWS, VT, DH), F32),
-            dma((6,)),
+            pltpu.SMEM((1,), F32),
+            pltpu.SMEM((4, 128), jnp.int32),
+            pltpu.SMEM((IMAGES,), jnp.int32),
+            dma((9,)),
             dma((1,)),
             dma((ND,)),
             dma((1,)),

time: 56.4 us -> 53.8 us (0.954)
  Pallas kernels: 54.2 us -> 52.4 us
  local copies, waits for them, and re-layouts: 1.32 us -> 0.61 us
    pallas_call x1, Pallas kernels: 54.2 us -> 52.4 us  [body(): pl.pallas_call(kernel, out_shape=pltpu.VMEM((ROWS, DH), BF16), in_specs=[...]
    unnamed x1, local copies, waits for them, and re-layouts: 1.32 us -> 0.61 us
where the time goes in v3:
time: 53.8 us; the launch traced here: 53.7 us
  Pallas kernels  52.4 us (97%)
  between operations  0.66 us (1%)
  local copies, waits for them, and re-layouts  0.61 us (1%)
    pallas_call x1, Pallas kernels, body(): pl.pallas_call(kernel, out_shape=pltpu.VMEM((ROWS, DH), BF16), in_specs=[...  52.4 us

profile of v3, /device:TPU:1, one launch (start us, length us, event | category | flops | bytes accessed | tf_op | source)
XLA Modules:
  0.0 53.7 jit_solution(15831663844981110337)
XLA Ops:
  0.7 52.4 %gated_cross_attention.1 = bf16[64,128]{1,0:T(8,128)(2,1)S(1)} custom-call(bf16[64,128]{1,0:T(8,128)(2,1)} %tok_h.1, f32[64,128]{1,0:T(8,128)} %bitcast.2, bf16[8192,128]{1,0:T(8,128)(2,1)} %wq_h.1, bf16[8192,128]{1,0:T(8,128)(2,1)} %wo_h.1, f32[1]{0:T(128)S(6)} %copy.12.gate_h, bf16[16,64,128]{2,1,0:T(8,128)(2,1)} %key_h.1, bf16[16,64,128]{2,1,0:T(8,128)(2,1)} %val_h.1, ...), custom_call_target="tpu_custom_call" | custom-call | tf_op jit(solution)/shard_map/gated_cross_attention/pallas_call | solution.py:321
  53.1 0.6 %copy.11 = bf16[64,128]{1,0:T(8,128)(2,1)} copy(bf16[64,128]{1,0:T(8,128)(2,1)S(1)} %gated_cross_attention.1) | data formatting | bytes 32768

commit v4 on v3

--- a/solution.py
+++ b/solution.py
@@ -18,7 +18,73 @@
 F32 = jnp.float32
 BF16 = jnp.bfloat16
 
-SPREAD = (
+NEAR_SPREAD = (
+    ((0, 0), ((0, 3), (0, 15), (1, 0), (0, 13), (3, 0), (0, 14))),
+    ((0, 15), ((3, 15), (0, 12), (2, 15), (0, 1))),
+    ((1, 0), ((1, 1),)),
+    ((3, 0), ((2, 0),)),
+    ((0, 3), ((0, 6), (1, 3), (2, 3))),
+    ((0, 14), ((1, 14), (3, 14), (2, 14))),
+    ((0, 13), ((3, 13), (0, 11), (2, 13), (1, 13), (0, 10))),
+    ((2, 0), ((2, 1),)),
+    ((2, 15), ((1, 15),)),
+    ((0, 1), ((0, 2), (3, 1))),
+    ((1, 3), ((1, 2), (1, 5), (1, 4), (3, 3))),
+    ((0, 12), ((2, 12), (1, 12), (3, 12))),
+    ((3, 13), ((3, 11),)),
+    ((0, 6), ((0, 8), (1, 6), (2, 6), (3, 6), (0, 5), (0, 7))),
+    ((0, 11), ((1, 11), (2, 11))),
+    ((2, 13), ((2, 10),)),
+    ((2, 1), ((2, 2),)),
+    ((0, 10), ((3, 10), (1, 10), (0, 9))),
+    ((0, 2), ((3, 2),)),
+    ((1, 4), ((2, 4), (0, 4))),
+    ((1, 5), ((2, 5), (3, 5))),
+    ((3, 3), ((3, 4),)),
+    ((2, 12), ((2, 9),)),
+    ((1, 6), ((1, 8), (1, 7))),
+    ((0, 7), ((3, 7),)),
+    ((0, 8), ((2, 8), (3, 8))),
+    ((2, 6), ((2, 7),)),
+    ((3, 10), ((3, 9),)),
+    ((0, 9), ((1, 9),)),
+    ((3, 15), ()),
+    ((1, 1), ()),
+    ((1, 14), ()),
+    ((3, 14), ()),
+    ((2, 3), ()),
+    ((1, 13), ()),
+    ((2, 14), ()),
+    ((1, 15), ()),
+    ((3, 1), ()),
+    ((1, 2), ()),
+    ((1, 12), ()),
+    ((3, 12), ()),
+    ((0, 5), ()),
+    ((1, 11), ()),
+    ((3, 6), ()),
+    ((3, 11), ()),
+    ((2, 2), ()),
+    ((1, 10), ()),
+    ((2, 11), ()),
+    ((3, 2), ()),
+    ((2, 4), ()),
+    ((2, 10), ()),
+    ((0, 4), ()),
+    ((2, 5), ()),
+    ((3, 4), ()),
+    ((3, 5), ()),
+    ((3, 7), ()),
+    ((1, 7), ()),
+    ((1, 8), ()),
+    ((3, 8), ()),
+    ((2, 9), ()),
+    ((2, 7), ()),
+    ((1, 9), ()),
+    ((3, 9), ()),
+    ((2, 8), ()),
+)
+FAR_SPREAD = (
     ((0, 0), ((0, 5), (0, 11), (1, 0), (0, 15), (3, 0), (2, 0), (0, 3))),
     ((1, 0), ((1, 1),)),
     ((3, 0), ((3, 13), (3, 1))),
@@ -27,33 +93,33 @@
     ((0, 3), ((2, 3), (0, 4), (3, 3), (0, 2), (1, 3))),
     ((0, 11), ((1, 11), (0, 8), (3, 11), (0, 10), (2, 11))),
     ((0, 5), ((0, 7), (1, 5), (3, 5), (2, 5), (0, 6))),
-    ((1, 1), ()),
     ((3, 1), ((2, 1),)),
-    ((1, 15), ()),
-    ((3, 15), ()),
     ((0, 14), ((1, 14), (3, 14))),
     ((2, 15), ((2, 14),)),
     ((0, 13), ((0, 12), (1, 13))),
-    ((0, 1), ()),
     ((3, 13), ((2, 13),)),
-    ((3, 3), ()),
     ((1, 3), ((1, 4), (1, 2))),
     ((0, 4), ((3, 4), (2, 4))),
-    ((0, 2), ()),
     ((2, 2), ((3, 2),)),
-    ((2, 3), ()),
     ((1, 11), ((1, 9), (1, 12))),
     ((3, 11), ((3, 9), (3, 12))),
     ((0, 10), ((1, 10), (3, 10))),
+    ((0, 6), ((3, 6),)),
     ((1, 5), ((1, 6),)),
-    ((0, 6), ((3, 6),)),
-    ((3, 5), ()),
     ((0, 7), ((1, 7), (2, 7), (3, 7))),
     ((2, 11), ((2, 9), (2, 10), (2, 12))),
+    ((0, 8), ((2, 8), (1, 8), (0, 9), (3, 8))),
+    ((2, 5), ((2, 6),)),
+    ((1, 1), ()),
+    ((1, 15), ()),
+    ((3, 15), ()),
+    ((0, 1), ()),
+    ((3, 3), ()),
+    ((0, 2), ()),
+    ((2, 3), ()),
+    ((3, 5), ()),
     ((2, 1), ()),
     ((1, 14), ()),
-    ((0, 8), ((2, 8), (1, 8), (0, 9), (3, 8))),
-    ((2, 5), ((2, 6),)),
     ((3, 14), ()),
     ((2, 14), ()),
     ((1, 13), ()),
@@ -129,7 +195,7 @@
         copy.start()
 
     barrier = pltpu.get_barrier_semaphore()
-    steps = {((c[0] - p[0]) % NY, (c[1] - p[1]) % NZ) for p, onward in SPREAD for c in onward}
+    steps = {((c[0] - p[0]) % NY, (c[1] - p[1]) % NZ) for p, onward in NEAR_SPREAD for c in onward}
     steps |= {((-a) % NY, (-b) % NZ) for a, b in steps}
     partners = [plane_peer(*step) for step in sorted(steps)]
     partners += [line_peer(1), line_peer(-1), sibling]
@@ -176,13 +242,12 @@
         for sem, (px, part) in enumerate(ARRIVED):
             kv_wait(which, images(px, False, part), 7 + sem)
 
-    index_of = {place: i for i, (place, _) in enumerate(SPREAD)}
-
     def arrived_block(place):
         return block(-place[0], -place[1])
 
-    def spread(buf, send_sem, recv_sem, i):
-        place, onward = SPREAD[i]
+    def spread(tree, buf, send_sem, recv_sem, i):
+        place, onward = tree[i]
+        index_of = {node: k for k, (node, _) in enumerate(tree)}
         here = buf.at[arrived_block(place)]
         if i > 0:
             pltpu.make_async_remote_copy(
@@ -199,7 +264,7 @@
         pltpu.make_async_copy(whole, whole, send_sem).wait()
 
     local[0].wait()
-    spread(tbuf, t_send.at[0], t_recv, 0)
+    spread(NEAR_SPREAD, tbuf, t_send.at[0], t_recv, 0)
     for which, parts in ((0, (0, 1)), (1, (0,))):
         for part in parts:
             kv_own_half(which, 1, part)
@@ -211,19 +276,19 @@
     total = own - shift
     square = total * total
     kv_steps = {
-        8: ((0, 0, 1), (0, 3, -1)),
-        26: ((0, 1, None), (0, 2, None)),
-        46: ((1, 0, 1), (1, 3, -1)),
-        63: ((0, 4, None), (0, 5, None)),
+        7: ((0, 0, 1), (0, 3, -1)),
+        15: ((0, 1, None), (0, 2, None)),
+        24: ((1, 0, 1), (1, 3, -1)),
+        54: ((0, 4, None), (0, 5, None)),
     }
     for i in range(1, ND):
-        spread(tbuf, t_send.at[0], t_recv, i)
-        part = tbuf[arrived_block(SPREAD[i][0])].astype(F32) - shift
+        spread(NEAR_SPREAD, tbuf, t_send.at[0], t_recv, i)
+        part = tbuf[arrived_block(NEAR_SPREAD[i][0])].astype(F32) - shift
         total = total + part
         square = square + part * part
         for which, sem, onward in kv_steps.get(i, ()):
             kv_arrive(which, sem, onward)
-        if i == 8:
+        if i == 7:
             kv_own_half(1, 1, 1)
             kv_own_half(1, -1, 0)
 
@@ -284,13 +349,13 @@
     lax.fori_loop(0, ROWS // 8, collect, 0)
     abuf[dp] = of[...].astype(BF16)
 
-    final = max(i for i, (_, onward) in enumerate(SPREAD) if onward) + 1
+    final = max(i for i, (_, onward) in enumerate(FAR_SPREAD) if onward) + 1
     for i in range(final):
-        spread(abuf, a_send.at[0], a_recv, i)
+        spread(FAR_SPREAD, abuf, a_send.at[0], a_recv, i)
     local[3].wait()
 
     def project_out(acc, first, last):
-        places = [arrived_block(SPREAD[i][0]) for i in range(first, last)]
+        places = [arrived_block(FAR_SPREAD[i][0]) for i in range(first, last)]
         lhs = jnp.concatenate([abuf[b] for b in places], axis=1)
         rhs = jnp.concatenate([wo[pl.ds(pl.multiple_of(b * DH, DH), DH), :] for b in places], axis=0)
         return acc + jnp.dot(lhs, rhs, preferred_element_type=F32)
@@ -301,7 +366,7 @@
     for first in range(final, ND, 4):
         last = min(first + 4, ND)
         for i in range(first, last):
-            spread(abuf, a_send.at[0], a_recv, i)
+            spread(FAR_SPREAD, abuf, a_send.at[0], a_recv, i)
         projected = project_out(projected, first, last)
     local[6].wait()
     gate = jnp.tanh(jnp.full((ROWS, DH), gate_s[0], F32))

time: 53.8 us -> 51.9 us (0.965)
  Pallas kernels: 52.4 us -> 50.5 us
    pallas_call x1, Pallas kernels: 52.4 us -> 50.5 us  [body(): pl.pallas_call(kernel, out_shape=pltpu.VMEM((ROWS, DH), BF16), in_specs=[...]
where the time goes in v4:
time: 51.9 us; the launch traced here: 51.8 us
  Pallas kernels  50.5 us (97%)
  between operations  0.66 us (1%)
  local copies, waits for them, and re-layouts  0.61 us (1%)
    pallas_call x1, Pallas kernels, body(): pl.pallas_call(kernel, out_shape=pltpu.VMEM((ROWS, DH), BF16), in_specs=[...  50.5 us

profile of v4, /device:TPU:1, one launch (start us, length us, event | category | flops | bytes accessed | tf_op | source)
XLA Modules:
  0.0 51.8 jit_solution(10321382555985605059)
XLA Ops:
  0.7 50.5 %gated_cross_attention.1 = bf16[64,128]{1,0:T(8,128)(2,1)S(1)} custom-call(bf16[64,128]{1,0:T(8,128)(2,1)} %tok_h.1, f32[64,128]{1,0:T(8,128)} %bitcast.2, bf16[8192,128]{1,0:T(8,128)(2,1)} %wq_h.1, bf16[8192,128]{1,0:T(8,128)(2,1)} %wo_h.1, f32[1]{0:T(128)S(6)} %copy.12.gate_h, bf16[16,64,128]{2,1,0:T(8,128)(2,1)} %key_h.1, bf16[16,64,128]{2,1,0:T(8,128)(2,1)} %val_h.1, ...), custom_call_target="tpu_custom_call" | custom-call | tf_op jit(solution)/shard_map/gated_cross_attention/pallas_call | solution.py:386
  51.1 0.6 %copy.11 = bf16[64,128]{1,0:T(8,128)(2,1)} copy(bf16[64,128]{1,0:T(8,128)(2,1)S(1)} %gated_cross_attention.1) | data formatting | bytes 32768

commit v5 on v3

--- a/solution.py
+++ b/solution.py
@@ -18,78 +18,144 @@
 F32 = jnp.float32
 BF16 = jnp.bfloat16
 
-SPREAD = (
-    ((0, 0), ((0, 5), (0, 11), (1, 0), (0, 15), (3, 0), (2, 0), (0, 3))),
-    ((1, 0), ((1, 1),)),
-    ((3, 0), ((3, 13), (3, 1))),
-    ((0, 15), ((0, 1), (2, 15), (1, 15), (0, 13), (0, 14), (3, 15))),
-    ((2, 0), ((2, 2),)),
-    ((0, 3), ((2, 3), (0, 4), (3, 3), (0, 2), (1, 3))),
-    ((0, 11), ((1, 11), (0, 8), (3, 11), (0, 10), (2, 11))),
-    ((0, 5), ((0, 7), (1, 5), (3, 5), (2, 5), (0, 6))),
+NEAR_SPREAD = (
+    ((0, 0), (((0, 0), (0, 14)), ((0, 0), (1, 0)), ((0, 0), (0, 2)), ((0, 0), (3, 0)), ((0, 0), (0, 1)))),
+    ((1, 0), (((1, 0), (1, 1)),)),
+    ((3, 0), (((3, 0), (2, 0)), ((3, 0), (3, 15)), ((3, 0), (3, 1)))),
+    ((0, 14), (((0, 14), (3, 14)), ((0, 14), (1, 14)))),
+    ((0, 2), (((0, 14), (0, 10)), ((0, 2), (0, 6)), ((0, 2), (0, 4)), ((0, 2), (2, 2)), ((0, 2), (3, 2)), ((0, 2), (1, 2)))),
+    ((1, 1), (((1, 1), (2, 1)),)),
+    ((3, 15), (((3, 15), (1, 15)), ((3, 15), (0, 15)), ((3, 15), (2, 15)))),
+    ((3, 1), (((3, 1), (3, 3)),)),
+    ((3, 14), (((3, 14), (3, 12)), ((3, 14), (3, 13)))),
+    ((1, 14), (((1, 14), (2, 14)), ((1, 14), (1, 13)))),
+    ((1, 2), (((1, 2), (1, 3)),)),
+    ((2, 2), (((2, 2), (2, 3)),)),
+    ((0, 4), (((0, 4), (0, 5)), ((0, 4), (3, 4)), ((0, 4), (1, 4)), ((0, 4), (0, 3)))),
+    ((0, 10), (((0, 10), (0, 8)), ((0, 10), (3, 10)), ((0, 10), (1, 10)), ((0, 10), (0, 11)), ((0, 10), (2, 10)))),
+    ((0, 6), (((0, 6), (0, 7)), ((0, 6), (0, 9)), ((0, 6), (2, 6)), ((0, 6), (3, 6)), ((0, 6), (1, 6)))),
+    ((2, 15), (((2, 15), (2, 13)),)),
+    ((2, 14), (((2, 14), (2, 11)),)),
+    ((1, 13), (((1, 13), (0, 13)), ((1, 13), (1, 12)))),
+    ((2, 3), (((2, 3), (2, 5)),)),
+    ((3, 12), (((3, 12), (0, 12)), ((3, 12), (2, 12)))),
+    ((3, 4), (((3, 4), (2, 4)),)),
+    ((0, 5), (((0, 5), (1, 5)), ((0, 5), (3, 5)))),
+    ((3, 10), (((3, 10), (3, 11)), ((3, 10), (3, 9)))),
+    ((1, 10), (((1, 10), (1, 9)),)),
+    ((0, 11), (((0, 11), (1, 11)),)),
+    ((0, 7), (((0, 7), (3, 7)),)),
+    ((0, 8), (((0, 8), (2, 8)), ((0, 8), (1, 8)), ((0, 8), (3, 8)))),
+    ((1, 6), (((1, 6), (1, 7)),)),
+    ((2, 10), (((2, 10), (2, 9)),)),
+    ((2, 6), (((2, 6), (2, 7)),)),
+    ((0, 1), ()),
+    ((2, 0), ()),
+    ((3, 2), ()),
+    ((2, 1), ()),
+    ((0, 15), ()),
+    ((1, 15), ()),
+    ((3, 3), ()),
+    ((3, 13), ()),
+    ((1, 3), ()),
+    ((1, 4), ()),
+    ((0, 3), ()),
+    ((3, 6), ()),
+    ((2, 13), ()),
+    ((0, 13), ()),
+    ((0, 9), ()),
+    ((1, 12), ()),
+    ((0, 12), ()),
+    ((2, 12), ()),
+    ((1, 5), ()),
+    ((2, 4), ()),
+    ((3, 11), ()),
+    ((3, 9), ()),
+    ((3, 5), ()),
+    ((1, 11), ()),
+    ((2, 5), ()),
+    ((2, 11), ()),
+    ((3, 7), ()),
+    ((1, 9), ()),
+    ((1, 7), ()),
+    ((3, 8), ()),
+    ((1, 8), ()),
+    ((2, 9), ()),
+    ((2, 7), ()),
+    ((2, 8), ()),
+)
+FAR_SPREAD = (
+    ((0, 0), (((0, 0), (0, 11)), ((0, 0), (3, 0)), ((0, 0), (2, 0)), ((0, 0), (0, 1)), ((0, 0), (0, 15)), ((0, 0), (0, 5)), ((0, 0), (0, 2)), ((0, 0), (1, 0)))),
+    ((3, 0), (((3, 0), (3, 13)),)),
+    ((0, 1), (((0, 1), (3, 1)), ((0, 1), (1, 1)))),
+    ((0, 15), (((0, 15), (2, 15)), ((0, 15), (0, 14)), ((0, 15), (3, 15)), ((0, 15), (1, 15)))),
+    ((1, 0), (((1, 0), (1, 3)), ((1, 0), (1, 14)))),
+    ((2, 0), (((2, 0), (2, 1)),)),
+    ((0, 2), (((0, 2), (2, 2)), ((0, 2), (0, 4)), ((0, 2), (3, 2)), ((0, 2), (1, 2)))),
+    ((0, 11), (((0, 11), (0, 8)), ((0, 11), (2, 11)), ((0, 11), (3, 11)), ((0, 11), (1, 11)), ((0, 11), (0, 9)), ((0, 11), (0, 12)))),
+    ((0, 5), (((0, 5), (2, 5)), ((0, 5), (1, 5)), ((0, 5), (0, 6)), ((0, 5), (3, 5)), ((0, 5), (0, 7)))),
+    ((0, 14), (((0, 14), (3, 14)),)),
+    ((2, 1), (((2, 1), (2, 4)),)),
+    ((1, 14), (((1, 14), (2, 14)), ((1, 14), (1, 13)), ((1, 14), (1, 12)))),
+    ((3, 13), (((3, 13), (2, 13)), ((3, 13), (3, 12)))),
+    ((1, 3), (((1, 3), (3, 3)), ((1, 3), (0, 3)))),
+    ((2, 2), (((2, 2), (2, 3)),)),
+    ((0, 4), (((0, 4), (1, 4)), ((0, 4), (3, 4)))),
+    ((1, 11), (((1, 11), (1, 10)),)),
+    ((0, 12), (((0, 12), (0, 13)),)),
+    ((3, 11), (((3, 11), (3, 10)),)),
+    ((0, 6), (((0, 6), (3, 6)), ((0, 6), (1, 6)))),
+    ((2, 11), (((2, 11), (2, 12)), ((2, 11), (2, 10)), ((2, 11), (2, 9)))),
+    ((0, 9), (((0, 9), (0, 10)), ((0, 9), (1, 9)), ((0, 9), (3, 9)))),
+    ((2, 5), (((2, 5), (2, 7)), ((2, 5), (2, 6)))),
+    ((0, 8), (((0, 8), (2, 8)), ((0, 8), (3, 8)), ((0, 8), (1, 8)))),
+    ((0, 7), (((0, 7), (3, 7)), ((0, 7), (1, 7)))),
+    ((3, 1), ()),
     ((1, 1), ()),
-    ((3, 1), ((2, 1),)),
     ((1, 15), ()),
     ((3, 15), ()),
-    ((0, 14), ((1, 14), (3, 14))),
-    ((2, 15), ((2, 14),)),
-    ((0, 13), ((0, 12), (1, 13))),
-    ((0, 1), ()),
-    ((3, 13), ((2, 13),)),
-    ((3, 3), ()),
-    ((1, 3), ((1, 4), (1, 2))),
-    ((0, 4), ((3, 4), (2, 4))),
-    ((0, 2), ()),
-    ((2, 2), ((3, 2),)),
-    ((2, 3), ()),
-    ((1, 11), ((1, 9), (1, 12))),
-    ((3, 11), ((3, 9), (3, 12))),
-    ((0, 10), ((1, 10), (3, 10))),
-    ((1, 5), ((1, 6),)),
-    ((0, 6), ((3, 6),)),
+    ((2, 15), ()),
+    ((1, 2), ()),
+    ((3, 2), ()),
+    ((1, 5), ()),
     ((3, 5), ()),
-    ((0, 7), ((1, 7), (2, 7), (3, 7))),
-    ((2, 11), ((2, 9), (2, 10), (2, 12))),
-    ((2, 1), ()),
-    ((1, 14), ()),
-    ((0, 8), ((2, 8), (1, 8), (0, 9), (3, 8))),
-    ((2, 5), ((2, 6),)),
     ((3, 14), ()),
     ((2, 14), ()),
     ((1, 13), ()),
-    ((0, 12), ()),
     ((2, 13), ()),
+    ((2, 3), ()),
+    ((0, 3), ()),
+    ((3, 12), ()),
     ((1, 4), ()),
-    ((1, 2), ()),
+    ((2, 4), ()),
     ((3, 4), ()),
-    ((3, 2), ()),
     ((1, 12), ()),
-    ((2, 4), ()),
-    ((3, 12), ()),
+    ((3, 3), ()),
+    ((0, 13), ()),
     ((1, 10), ()),
+    ((3, 6), ()),
+    ((1, 6), ()),
     ((3, 10), ()),
+    ((2, 12), ()),
+    ((2, 10), ()),
+    ((0, 10), ()),
     ((1, 9), ()),
-    ((1, 6), ()),
-    ((3, 6), ()),
+    ((3, 9), ()),
+    ((3, 8), ()),
+    ((1, 8), ()),
+    ((2, 6), ()),
+    ((3, 7), ()),
+    ((2, 9), ()),
     ((1, 7), ()),
-    ((3, 9), ()),
-    ((2, 12), ()),
-    ((3, 7), ()),
-    ((0, 9), ()),
-    ((1, 8), ()),
-    ((2, 10), ()),
-    ((2, 6), ()),
-    ((3, 8), ()),
     ((2, 7), ()),
     ((2, 8), ()),
-    ((2, 9), ()),
 )
 
 
 def kernel(
     tok_h, gain_h, wq_h, wo_h, gate_h, key_h, val_h, act_h, slot_h,
     out_ref,
-    tbuf, abuf, wq, wo, gain, kbuf, vbuf, qf, of, pbuf, gate_s, act_s, slot_s,
+    tbuf, abuf, wq, wo, gain, kbuf, vbuf, of, pbuf, gate_s, act_s, slot_s,
     local_sem, t_send, t_recv, a_send, a_recv, kv_send, kv_recv,
 ):
     dp = lax.axis_index("dp")
@@ -125,11 +191,10 @@
             (slot_h, slot_s),
         ))
     ]
-    for copy in local:
-        copy.start()
+    local[0].start()
 
     barrier = pltpu.get_barrier_semaphore()
-    steps = {((c[0] - p[0]) % NY, (c[1] - p[1]) % NZ) for p, onward in SPREAD for c in onward}
+    steps = {(a % NY, b % NZ) for _, (a, b) in NEAR_SPREAD[0][1]}
     steps |= {((-a) % NY, (-b) % NZ) for a, b in steps}
     partners = [plane_peer(*step) for step in sorted(steps)]
     partners += [line_peer(1), line_peer(-1), sibling]
@@ -176,54 +241,56 @@
         for sem, (px, part) in enumerate(ARRIVED):
             kv_wait(which, images(px, False, part), 7 + sem)
 
-    index_of = {place: i for i, (place, _) in enumerate(SPREAD)}
-
     def arrived_block(place):
         return block(-place[0], -place[1])
 
-    def spread(buf, send_sem, recv_sem, i):
-        place, onward = SPREAD[i]
+    def spread(tree, buf, send_sem, recv_sem, i):
+        place, onward = tree[i]
+        index_of = {node: k for k, (node, _) in enumerate(tree)}
         here = buf.at[arrived_block(place)]
         if i > 0:
             pltpu.make_async_remote_copy(
                 src_ref=here, dst_ref=here, send_sem=send_sem, recv_sem=recv_sem.at[i],
                 device_id=sibling, device_id_type=MESH).wait_recv()
-        for target in onward:
+        for origin, target in onward:
+            here = buf.at[arrived_block(origin)]
             pltpu.make_async_remote_copy(
                 src_ref=here, dst_ref=here, send_sem=send_sem, recv_sem=recv_sem.at[index_of[target]],
-                device_id=plane_peer(target[0] - place[0], target[1] - place[1]),
+                device_id=plane_peer(target[0] - origin[0], target[1] - origin[1]),
                 device_id_type=MESH).start()
 
     def all_sent(buf, send_sem):
         whole = buf.at[pl.ds(0, ND - 1)]
         pltpu.make_async_copy(whole, whole, send_sem).wait()
 
-    local[0].wait()
-    spread(tbuf, t_send.at[0], t_recv, 0)
     for which, parts in ((0, (0, 1)), (1, (0,))):
         for part in parts:
             kv_own_half(which, 1, part)
             kv_own_half(which, -1, 1 - part)
         kv_own_sibling(which)
+    local[0].wait()
+    spread(NEAR_SPREAD, tbuf, t_send.at[0], t_recv, 0)
+    for i in range(1, 9):
+        local[i].start()
 
     own = tbuf[dp].astype(F32)
     shift = jnp.broadcast_to(jnp.sum(own, axis=1, keepdims=True) * (1.0 / DH), (ROWS, DH))
     total = own - shift
     square = total * total
     kv_steps = {
-        8: ((0, 0, 1), (0, 3, -1)),
-        26: ((0, 1, None), (0, 2, None)),
-        46: ((1, 0, 1), (1, 3, -1)),
-        63: ((0, 4, None), (0, 5, None)),
+        5: ((0, 0, 1), (0, 3, -1)),
+        15: ((0, 1, None), (0, 2, None)),
+        25: ((1, 0, 1), (1, 3, -1)),
+        50: ((0, 4, None), (0, 5, None)),
     }
     for i in range(1, ND):
-        spread(tbuf, t_send.at[0], t_recv, i)
-        part = tbuf[arrived_block(SPREAD[i][0])].astype(F32) - shift
+        spread(NEAR_SPREAD, tbuf, t_send.at[0], t_recv, i)
+        part = tbuf[arrived_block(NEAR_SPREAD[i][0])].astype(F32) - shift
         total = total + part
         square = square + part * part
         for which, sem, onward in kv_steps.get(i, ()):
             kv_arrive(which, sem, onward)
-        if i == 8:
+        if i == 5:
             kv_own_half(1, 1, 1)
             kv_own_half(1, -1, 0)
 
@@ -245,7 +312,7 @@
         return acc + jnp.dot(lhs, rhs, preferred_element_type=F32)
 
     queries = lax.fori_loop(0, ND // 4, project, jnp.zeros((ROWS, DH), F32), unroll=4)
-    qf[...] = queries.astype(BF16).astype(F32)
+    queries_b = queries.astype(BF16)
 
     kv_arrive(1, 1)
     kv_arrive(1, 2)
@@ -257,16 +324,20 @@
         image = act_s[j % 4, mp * (ROWS // 4) + i * 2 + j // 4]
         return slot_s[image]
 
-    def weigh(i, carry):
+    lane = lax.broadcasted_iota(jnp.int32, (VT, ROWS), 1)
+
+    def score(i, acc):
+        keys = jnp.concatenate([kbuf[slot_of(i, j)] for j in range(8)], axis=0)
+        each = lax.dot_general(keys, queries_b, (((1,), (1,)), ((), ())), preferred_element_type=F32)
         for j in range(8):
-            q = qf[pl.ds(i * 8 + j, 1), :]
-            s = jnp.sum(kbuf[slot_of(i, j)].astype(F32) * q, axis=1, keepdims=True) * (DH ** -0.5)
-            e = jnp.exp(s - jnp.max(s, axis=0, keepdims=True))
-            p = (e / jnp.sum(e, axis=0, keepdims=True)).astype(BF16).astype(F32)
-            pbuf[i * 8 + j] = jnp.broadcast_to(p, (VT, DH))
-        return carry
-
-    lax.fori_loop(0, ROWS // 8, weigh, 0)
+            acc = jnp.where(lane == i * 8 + j, each[j * VT:(j + 1) * VT], acc)
+        return acc
+
+    s = lax.fori_loop(0, ROWS // 8, score, jnp.zeros((VT, ROWS), F32)) * (DH ** -0.5)
+    e = jnp.exp(s - jnp.max(s, axis=0, keepdims=True))
+    p = (e / jnp.sum(e, axis=0, keepdims=True)).astype(BF16).astype(F32)
+    for r in range(ROWS):
+        pbuf[r] = jnp.broadcast_to(p[:, r:r + 1], (VT, DH))
 
     kv_arrive(1, 4)
     kv_arrive(1, 5)
@@ -284,13 +355,13 @@
     lax.fori_loop(0, ROWS // 8, collect, 0)
     abuf[dp] = of[...].astype(BF16)
 
-    final = max(i for i, (_, onward) in enumerate(SPREAD) if onward) + 1
+    final = max(i for i, (_, onward) in enumerate(FAR_SPREAD) if onward) + 1
     for i in range(final):
-        spread(abuf, a_send.at[0], a_recv, i)
+        spread(FAR_SPREAD, abuf, a_send.at[0], a_recv, i)
     local[3].wait()
 
     def project_out(acc, first, last):
-        places = [arrived_block(SPREAD[i][0]) for i in range(first, last)]
+        places = [arrived_block(FAR_SPREAD[i][0]) for i in range(first, last)]
         lhs = jnp.concatenate([abuf[b] for b in places], axis=1)
         rhs = jnp.concatenate([wo[pl.ds(pl.multiple_of(b * DH, DH), DH), :] for b in places], axis=0)
         return acc + jnp.dot(lhs, rhs, preferred_element_type=F32)
@@ -301,7 +372,7 @@
     for first in range(final, ND, 4):
         last = min(first + 4, ND)
         for i in range(first, last):
-            spread(abuf, a_send.at[0], a_recv, i)
+            spread(FAR_SPREAD, abuf, a_send.at[0], a_recv, i)
         projected = project_out(projected, first, last)
     local[6].wait()
     gate = jnp.tanh(jnp.full((ROWS, DH), gate_s[0], F32))
@@ -331,7 +402,6 @@
             pltpu.VMEM((ND, DH), F32),
             pltpu.VMEM((IMAGES, VT, DH), BF16),
             pltpu.VMEM((IMAGES, VT, DH), BF16),
-            pltpu.VMEM((ROWS, DH), F32),
             pltpu.VMEM((ROWS, DH), F32),
             pltpu.VMEM((ROWS, VT, DH), F32),
             pltpu.SMEM((1,), F32),

time: 53.8 us -> 51.5 us (0.957)
  Pallas kernels: 52.4 us -> 50.1 us
    pallas_call x1, Pallas kernels: 52.4 us -> 50.1 us  [body(): pl.pallas_call(kernel, out_shape=pltpu.VMEM((ROWS, DH), BF16), in_specs=[...]
where the time goes in v5:
time: 51.5 us; the launch traced here: 51.4 us
  Pallas kernels  50.1 us (97%)
  between operations  0.66 us (1%)
  local copies, waits for them, and re-layouts  0.61 us (1%)
    pallas_call x1, Pallas kernels, body(): pl.pallas_call(kernel, out_shape=pltpu.VMEM((ROWS, DH), BF16), in_specs=[...  50.1 us

profile of v5, /device:TPU:1, one launch (start us, length us, event | category | flops | bytes accessed | tf_op | source)
XLA Modules:
  0.0 51.4 jit_solution(14984889650957971936)
XLA Ops:
  0.7 50.1 %gated_cross_attention.1 = bf16[64,128]{1,0:T(8,128)(2,1)S(1)} custom-call(bf16[64,128]{1,0:T(8,128)(2,1)} %tok_h.1, f32[64,128]{1,0:T(8,128)} %bitcast.2, bf16[8192,128]{1,0:T(8,128)(2,1)} %wq_h.1, bf16[8192,128]{1,0:T(8,128)(2,1)} %wo_h.1, f32[1]{0:T(128)S(6)} %copy.12.gate_h, bf16[16,64,128]{2,1,0:T(8,128)(2,1)} %key_h.1, bf16[16,64,128]{2,1,0:T(8,128)(2,1)} %val_h.1, ...), custom_call_target="tpu_custom_call" | custom-call | tf_op jit(solution)/shard_map/gated_cross_attention/pallas_call | solution.py:392
  50.8 0.6 %copy.11 = bf16[64,128]{1,0:T(8,128)(2,1)} copy(bf16[64,128]{1,0:T(8,128)(2,1)S(1)} %gated_cross_attention.1) | data formatting | bytes 32768

commit v6 on v5

--- a/solution.py
+++ b/solution.py
@@ -369,13 +369,13 @@
     projected = jnp.zeros((ROWS, DH), F32)
     for first in range(0, final, 8):
         projected = project_out(projected, first, min(first + 8, final))
-    for first in range(final, ND, 4):
-        last = min(first + 4, ND)
+    local[6].wait()
+    gate = jnp.tanh(jnp.full((ROWS, DH), gate_s[0], F32))
+    cuts = [*range(final, ND - 2, 6), ND - 2, ND]
+    for first, last in zip(cuts, cuts[1:]):
         for i in range(first, last):
             spread(FAR_SPREAD, abuf, a_send.at[0], a_recv, i)
         projected = project_out(projected, first, last)
-    local[6].wait()
-    gate = jnp.tanh(jnp.full((ROWS, DH), gate_s[0], F32))
     out_ref[...] = (tbuf[dp].astype(F32) + gate * projected).astype(BF16)
 
     all_sent(tbuf, t_send.at[0])

time: 51.5 us -> 51.7 us (level)
  no operation moved by 1% of the time
where the time goes in v6:
time: 51.7 us; the launch traced here: 51.5 us
  Pallas kernels  50.3 us (97%)
  between operations  0.66 us (1%)
  local copies, waits for them, and re-layouts  0.61 us (1%)
    pallas_call x1, Pallas kernels, body(): pl.pallas_call(kernel, out_shape=pltpu.VMEM((ROWS, DH), BF16), in_specs=[...  50.3 us

profile of v6, /device:TPU:1, one launch (start us, length us, event | category | flops | bytes accessed | tf_op | source)
XLA Modules:
  0.0 51.5 jit_solution(565451453245438752)
XLA Ops:
  0.7 50.3 %gated_cross_attention.1 = bf16[64,128]{1,0:T(8,128)(2,1)S(1)} custom-call(bf16[64,128]{1,0:T(8,128)(2,1)} %tok_h.1, f32[64,128]{1,0:T(8,128)} %bitcast.2, bf16[8192,128]{1,0:T(8,128)(2,1)} %wq_h.1, bf16[8192,128]{1,0:T(8,128)(2,1)} %wo_h.1, f32[1]{0:T(128)S(6)} %copy.12.gate_h, bf16[16,64,128]{2,1,0:T(8,128)(2,1)} %key_h.1, bf16[16,64,128]{2,1,0:T(8,128)(2,1)} %val_h.1, ...), custom_call_target="tpu_custom_call" | custom-call | tf_op jit(solution)/shard_map/gated_cross_attention/pallas_call | solution.py:392
  50.9 0.6 %copy.11 = bf16[64,128]{1,0:T(8,128)(2,1)} copy(bf16[64,128]{1,0:T(8,128)(2,1)S(1)} %gated_cross_attention.1) | data formatting | bytes 32768
